TPU v7x, 32 devices: a whole 2x2x4 slice. The times are simulated.
32 devices in a mesh: wide: 8 (over y, x, core), narrow: 4 (over z).
Axes of the slice: x: 2, y: 2, z: 4, core: 2. Of those that a mesh axis runs over, the one named last changes fastest.
Arguments:
- local_slopes: float32 [32, 512, 128], P(('wide', 'narrow')), may hold values from -0.25 to 0.25
- global_slopes: float32 [32, 512, 1024], P(('wide', 'narrow')), may hold values from -0.25 to 0.25
- residuals: float32 [32, 512], P(('wide', 'narrow')), may hold values from -6 to 6
- weights: float32 [32, 512], P(('wide', 'narrow')), may hold values from 0.1 to 10
- track_slot_count: int32 [32], P(('wide', 'narrow')), may hold values from 64 to 512
- windows: int32 [32], P(('wide', 'narrow')), may hold values from 0 to 3
Outputs:
- normal_matrix: float32 [4, 1024, 1024], P(None, 'narrow', 'wide')
- normal_rhs: float32 [4, 1024], P(None, 'narrow')
All inputs are finite; a program needn't handle non-finite values.
Results may differ from a plain program's by a relative error of at most 0.0003.
Values sent between devices are 32-bit elements; how exact they have to be, the bound alone decides.
A program may use at most 64 MiB of HBM per device.

v0:
```python
import jax
import jax.numpy as jnp
from jax import lax
from jax.sharding import PartitionSpec as P

WINDOW_PARAMS = 1024
NWIN = 4


def tdot(left, right):
    return lax.dot_general(
        left,
        right,
        (((0,), (0,)), ((), ())),
        precision=lax.Precision.HIGHEST,
        preferred_element_type=jnp.float32,
    )


def rows_product(left, right):
    return tdot(left, right)


def window_sum(window_ids, stacked):
    picks = (window_ids[:, None] == jnp.arange(NWIN, dtype=jnp.int32)[None, :]).astype(jnp.float32)
    return jnp.einsum(
        "bw,bij->wij",
        picks,
        stacked,
        precision=lax.Precision.HIGHEST,
        preferred_element_type=jnp.float32,
    )


def on_device(local_slopes, global_slopes, residuals, weights, track_slot_count, windows):
    bundle_count, measure_slot, local_param = local_slopes.shape
    slot_entries = jnp.arange(measure_slot, dtype=jnp.int32)
    count = track_slot_count[0]
    local_b = local_slopes[0]
    global_b = global_slopes[0]
    resid_b = residuals[0][:, None]
    live = jnp.where(slot_entries < count, weights[0], jnp.float32(0.0))
    wl = local_b * live[:, None]
    wg = global_b * live[:, None]
    curv = rows_product(wl, local_b) + jnp.eye(local_param, dtype=jnp.float32)
    lr = rows_product(wl, resid_b)
    gr = rows_product(wg, resid_b)[:, 0]
    coupling = rows_product(wl, global_b)
    gram = rows_product(wg, global_b)
    factor = jnp.linalg.cholesky(curv)
    solved = jax.scipy.linalg.cho_solve((factor, True), jnp.concatenate([coupling, lr], axis=1))
    schurs = [gram - tdot(coupling, solved[:, :WINDOW_PARAMS])]
    reduced = [gr - tdot(coupling, solved[:, WINDOW_PARAMS:])[:, 0]]
    stacked = jnp.stack(schurs, axis=0)
    rhs_stack = jnp.stack(reduced, axis=0)
    rhs_local = window_sum(windows, rhs_stack[:, :, None])[:, :, 0]
    rhs_whole = lax.psum(rhs_local, ("wide", "narrow"))
    owned = WINDOW_PARAMS // lax.axis_size("narrow")
    normal_rhs = lax.dynamic_slice_in_dim(rhs_whole, lax.axis_index("narrow") * owned, owned, 1)
    received = lax.all_to_all(stacked, "wide", split_axis=2, concat_axis=0, tiled=True)
    window_ids = lax.all_gather(windows, "wide", axis=0, tiled=True)
    partial_value = window_sum(window_ids, received)
    normal_matrix = lax.psum_scatter(partial_value, "narrow", scatter_dimension=1, tiled=True)
    return (normal_matrix, normal_rhs)


def solution(mesh):
    in_specs = (
        P(("wide", "narrow"), None, None),
        P(("wide", "narrow"), None, None),
        P(("wide", "narrow"), None),
        P(("wide", "narrow"), None),
        P(("wide", "narrow")),
        P(("wide", "narrow")),
    )
    out_specs = (P(None, "narrow", "wide"), P(None, "narrow"))
    return jax.shard_map(
        on_device, mesh=mesh, in_specs=in_specs, out_specs=out_specs, check_vma=False
    )
```

profile of v0, /device:TPU:0, one launch (start us, length us, event | category | flops | bytes accessed | tf_op | source)
XLA Modules:
  0.0 232.3 jit_solution(12225820016373866067)
XLA Ops:
  7.8 0.7 fusion.39
  8.5 1.7 fusion.18
  10.4 11.7 %cholesky.17 = f32[128,128]{1,0:T(8,128)S(1)} custom-call(f32[128,128]{1,0:T(8,128)S(1)} %fusion.34), custom_call_target="Cholesky" | custom-call | tf_op jit(solution)/shard_map/jit(cholesky)/cholesky | solution.py:50
  22.1 0.6 compare_reduce_fusion
  22.8 0.7 fusion.29
  23.4 9.8 %custom-call.10 = f32[1,128,128]{1,2,0:T(8,128)S(1)} custom-call(f32[1,128,128]{2,1,0:T(8,128)S(1)} %fusion.29), custom_call_target="InvertDiagBlocksLowerTriangular" | custom-call | tf_op jit(solution)/shard_map/jit(_cho_solve)/triangular_solve | solution.py:51
  33.3 1.6 convolution_bitcast_fusion
  34.9 3.1 %fusion.2 = f32[128,1024]{1,0:T(8,128)S(1)} fusion(f32[1,512,1024]{2,1,0:T(8,128)} %param.7, f32[1,512,128]{2,1,0:T(8,128)} %param.6, f32[512]{0:T(512)S(1)} %fusion.39), kind=kOutput, calls=%fused_computation.3 | convolution fusion | flops 805371904 | bytes 2885632 | tf_op jit(solution)/shard_map/dot_general | solution.py:11
  38.0 0.7 fusion.12
  38.7 1.1 fusion.30
  39.8 3.7 %fusion.16 = f32[1024,1024]{1,0:T(8,128)S(1)} fusion(f32[128,1024]{1,0:T(8,128)S(1)} %fusion.2, f32[128,1025]{0,1:T(8,128)S(1)} %fusion.30), kind=kOutput, calls=%fused_computation.18 | convolution fusion | flops 1610612736 | bytes 5242880 | tf_op jit(solution)/shard_map/dot_general | solution.py:11
  43.5 8.7 %subtract_bitcast_fusion = f32[1,1024,1024]{2,1,0:T(8,128)} fusion(f32[1024,1024]{1,0:T(8,128)S(1)} %fusion.16, f32[1,512,1024]{2,1,0:T(8,128)S(1)} %copy-done.1, f32[512]{0:T(512)S(1)} %fusion.39), kind=kOutput, calls=%fused_computation.2 | convolution fusion | flops 6444023808 | bytes 10487808 | tf_op jit(solution)/shard_map/dot_general | solution.py:11
  52.2 11.0 %copy.13 = f32[1,1024,1024]{1,0,2:T(1,128)} copy(f32[1,1024,1024]{2,1,0:T(8,128)} %subtract_bitcast_fusion) | data formatting | bytes 8388608 | tf_op jit(solution)/shard_map/stack | solution.py:54
  63.2 5.3 %all-to-all-start = ((f32[1,1024,1024]{1,0,2:T(1,128)}), f32[1,1024,1024]{1,0,2:T(1,128)}, u32[]{:S(2)}, u32[]{:S(2)}) async-start(f32[1,1024,1024]{1,0,2:T(1,128)} %copy.13), calls=%async_computation | async-start | bytes 8388608 | tf_op jit(solution)/shard_map/all_to_all | solution.py:60
  69.8 0.8 dynamic-update-slice.3
  70.6 49.3 %all-reduce = s32[8]{0:T(128)S(1)} all-reduce(s32[8]{0:T(128)S(1)} %dynamic-update-slice.3), channel_id=1, replica_groups=mesh['wide'=8,'narrow'=4] {'wide'}, use_global_device_ids=true, to_apply=%add | all-reduce | flops 8 | bytes 64
  119.9 5.2 %copy.17 = f32[1,1024,1024]{1,2,0:T(8,128)} copy(f32[1,1024,1024]{1,0,2:T(1,128)} %all-to-all-done) | data formatting | bytes 8388608
  125.0 5.4 %copy.16 = f32[1,1024,8,128]{3,2,1,0:T(8,128)} copy(f32[1,1024,8,128]{1,3,2,0:T(8,128)} %bitcast.68) | data formatting | bytes 8388608 | tf_op jit(solution)/shard_map/all_to_all | solution.py:60
  130.4 5.6 %fusion = f32[4,1024,128]{2,0,1:T(4,128)} fusion(f32[1,1024,8,128]{3,2,1,0:T(8,128)} %copy.16, s32[8]{0:T(128)S(1)} %all-reduce), kind=kOutput, calls=%fused_computation | convolution fusion | flops 50331680 | bytes 6291488 | tf_op jit(solution)/shard_map/bw,bij->wij/dot_general | solution.py:26
  138.3 1.3 fusion.5
  139.7 42.9 %psum.7 = f32[4,1024]{1,0:T(4,128)S(1)} all-reduce(f32[4,1024]{1,0:T(4,128)S(1)} %broadcast_multiply_fusion), channel_id=1, replica_groups=mesh['wide'=8,'narrow'=4] {'wide','narrow'}, use_global_device_ids=true, to_apply=%region_3.4 | all-reduce | flops 4096 | bytes 32768 | tf_op jit(solution)/shard_map/psum | solution.py:57
  183.1 40.4 %all-reduce.4.cloned.1.call-done = f32[4,1024,128]{2,0,1:T(4,128)} async-done(((f32[4,1024,128]{2,0,1:T(4,128)}), f32[4,1024,128]{2,0,1:T(4,128)}) %all-reduce.4.cloned.1.call-update) | async-done | bytes 2097168
  223.5 1.1 constant_dynamic-slice_fusion
  224.6 0.8 copy.15
  (22 shorter events, 3.1 us)
Async XLA Ops:
  7.2 26.1 %copy-start = (f32[1,512]{1,0:T(1,128)S(1)}, f32[1,512]{1,0:T(1,128)}, u32[]{:S(2)}) copy-start(f32[1,512]{1,0:T(1,128)} %param.8) | copy-start | bytes 6148
  39.8 3.7 %copy-start.1 = (f32[1,512,1024]{2,1,0:T(8,128)S(1)}, f32[1,512,1024]{2,1,0:T(8,128)}, u32[]{:S(2)}) copy-start(f32[1,512,1024]{2,1,0:T(8,128)} %param.7) | copy-start | bytes 6291460
  63.2 6.0 %copy-start.3 = (u32[32]{0:T(128)S(1)}, u32[32]{0:T(128)}, u32[]{:S(2)}) copy-start(u32[32]{0:T(128)} %constant.68) | copy-start | bytes 388
  63.2 56.7 %all-to-all-start = ((f32[1,1024,1024]{1,0,2:T(1,128)}), f32[1,1024,1024]{1,0,2:T(1,128)}, u32[]{:S(2)}, u32[]{:S(2)}) async-start(f32[1,1024,1024]{1,0,2:T(1,128)} %copy.13), calls=%async_computation | async-start | bytes 8388608 | tf_op jit(solution)/shard_map/all_to_all | solution.py:60
  68.5 155.0 %all-reduce.4.cloned.1.call-start = ((), (), s32[]{:S(2)}) async-start(), calls=%async_computation.1 | async-start | bytes 4194304
  136.0 0.7 copy-start.2
Sparse Core Ops, SparseCore 0:
  136.1 87.3 all-reduce.3
where the time goes:
time: 233 us; the launch traced here: 232 us
  blocking collectives  92.2 us (40%)
  waiting for transfers between devices  40.4 us (17%)
  matrix products  27.9 us (12%)
  local copies, waits for them, and re-layouts  26.7 us (11%)
  other arithmetic  23.6 us (10%)
  between operations  16.1 us (7%)
  starting transfers between devices  5.37 us (2%)
    unnamed x1, blocking collectives  49.3 us
    psum x1, blocking collectives, on_device(): rhs_whole = lax.psum(rhs_local, ('wide', 'narrow'))  42.9 us
    unnamed x2, waiting for transfers between devices  40.4 us
    dot_general x7, matrix products, tdot(): lax.dot_general(left, right, (((0,), (0,)), ((), ())), precision=lax.Prec...  20.5 us
    another operation x3, other arithmetic, on_device(): factor = jnp.linalg.cholesky(curv)  12.4 us
    another operation x1, local copies, waits for them, and re-layouts, on_device(): stacked = jnp.stack(schurs, axis=0)  11 us
    another operation x2, other arithmetic, on_device(): jax.scipy.linalg.cho_solve((factor, True), jnp.concatenate([coupling, lr]...  10.5 us
    unnamed x15, local copies, waits for them, and re-layouts  9.63 us
  transfers between devices with their start and end apart: 2, of which 1 were waited for; matrix products, arithmetic and copies ran while one was open for 2% of the time, Pallas kernels for 0%

commit v1 on v0

--- a/solution.py
+++ b/solution.py
@@ -54,7 +54,7 @@
     stacked = jnp.stack(schurs, axis=0)
     rhs_stack = jnp.stack(reduced, axis=0)
     rhs_local = window_sum(windows, rhs_stack[:, :, None])[:, :, 0]
-    rhs_whole = lax.psum(rhs_local, ("wide", "narrow"))
+    rhs_whole = jnp.sum(lax.all_gather(rhs_local, ("wide", "narrow")), axis=0)
     owned = WINDOW_PARAMS // lax.axis_size("narrow")
     normal_rhs = lax.dynamic_slice_in_dim(rhs_whole, lax.axis_index("narrow") * owned, owned, 1)
     received = lax.all_to_all(stacked, "wide", split_axis=2, concat_axis=0, tiled=True)

time: 233 us -> 241 us (1.034)
  blocking collectives: 92.2 us -> 129 us
  waiting for transfers between devices: 40.4 us -> 11.3 us
    all_gather x0 -> x1, blocking collectives: none -> 79.8 us  [on_device(): rhs_whole = jnp.sum(lax.all_gather(rhs_local, ('wide', 'narrow')), axis=0)]
    psum x1 -> x0, blocking collectives: 42.9 us -> none  [on_device(): rhs_whole = lax.psum(rhs_local, ('wide', 'narrow'))]
    unnamed x2, waiting for transfers between devices: 40.4 us -> 11.3 us
where the time goes in v1:
time: 241 us; the launch traced here: 240 us
  blocking collectives  129 us (54%)
  matrix products  27.9 us (12%)
  local copies, waits for them, and re-layouts  26.7 us (11%)
  other arithmetic  23.7 us (10%)
  between operations  16.1 us (7%)
  waiting for transfers between devices  11.3 us (5%)
  starting transfers between devices  5.37 us (2%)
    all_gather x1, blocking collectives, on_device(): rhs_whole = jnp.sum(lax.all_gather(rhs_local, ('wide', 'narrow')), axis=0)  79.8 us
    unnamed x1, blocking collectives  49.3 us
    dot_general x7, matrix products, tdot(): lax.dot_general(left, right, (((0,), (0,)), ((), ())), precision=lax.Prec...  20.5 us
    another operation x3, other arithmetic, on_device(): factor = jnp.linalg.cholesky(curv)  12.4 us
    unnamed x2, waiting for transfers between devices  11.3 us
    another operation x1, local copies, waits for them, and re-layouts, on_device(): stacked = jnp.stack(schurs, axis=0)  11 us
    another operation x2, other arithmetic, on_device(): jax.scipy.linalg.cho_solve((factor, True), jnp.concatenate([coupling, lr]...  10.5 us
    unnamed x15, local copies, waits for them, and re-layouts  9.63 us
  transfers between devices with their start and end apart: 2, of which 1 were waited for; matrix products, arithmetic and copies ran while one was open for 2% of the time, Pallas kernels for 0%

profile of v1, /device:TPU:0, one launch (start us, length us, event | category | flops | bytes accessed | tf_op | source)
XLA Modules:
  0.0 240.2 jit_solution(18207338409751753867)
XLA Ops:
  7.8 0.7 fusion.39
  8.5 1.7 fusion.18
  10.4 11.7 %cholesky.17 = f32[128,128]{1,0:T(8,128)S(1)} custom-call(f32[128,128]{1,0:T(8,128)S(1)} %fusion.34), custom_call_target="Cholesky" | custom-call | tf_op jit(solution)/shard_map/jit(cholesky)/cholesky | solution.py:50
  22.1 0.6 compare_reduce_fusion
  22.8 0.7 fusion.29
  23.4 9.8 %custom-call.10 = f32[1,128,128]{1,2,0:T(8,128)S(1)} custom-call(f32[1,128,128]{2,1,0:T(8,128)S(1)} %fusion.29), custom_call_target="InvertDiagBlocksLowerTriangular" | custom-call | tf_op jit(solution)/shard_map/jit(_cho_solve)/triangular_solve | solution.py:51
  33.3 1.6 convolution_bitcast_fusion
  34.9 3.1 %fusion.2 = f32[128,1024]{1,0:T(8,128)S(1)} fusion(f32[1,512,1024]{2,1,0:T(8,128)} %param.7, f32[1,512,128]{2,1,0:T(8,128)} %param.6, f32[512]{0:T(512)S(1)} %fusion.39), kind=kOutput, calls=%fused_computation.3 | convolution fusion | flops 805371904 | bytes 2885632 | tf_op jit(solution)/shard_map/dot_general | solution.py:11
  38.0 0.7 fusion.12
  38.7 1.1 fusion.30
  39.8 3.7 %fusion.16 = f32[1024,1024]{1,0:T(8,128)S(1)} fusion(f32[128,1024]{1,0:T(8,128)S(1)} %fusion.2, f32[128,1025]{0,1:T(8,128)S(1)} %fusion.30), kind=kOutput, calls=%fused_computation.18 | convolution fusion | flops 1610612736 | bytes 5242880 | tf_op jit(solution)/shard_map/dot_general | solution.py:11
  43.5 8.7 %subtract_bitcast_fusion = f32[1,1024,1024]{2,1,0:T(8,128)} fusion(f32[1024,1024]{1,0:T(8,128)S(1)} %fusion.16, f32[1,512,1024]{2,1,0:T(8,128)S(1)} %copy-done.1, f32[512]{0:T(512)S(1)} %fusion.39), kind=kOutput, calls=%fused_computation.2 | convolution fusion | flops 6444023808 | bytes 10487808 | tf_op jit(solution)/shard_map/dot_general | solution.py:11
  52.2 11.0 %copy.13 = f32[1,1024,1024]{1,0,2:T(1,128)} copy(f32[1,1024,1024]{2,1,0:T(8,128)} %subtract_bitcast_fusion) | data formatting | bytes 8388608 | tf_op jit(solution)/shard_map/stack | solution.py:54
  63.2 5.3 %all-to-all-start = ((f32[1,1024,1024]{1,0,2:T(1,128)}), f32[1,1024,1024]{1,0,2:T(1,128)}, u32[]{:S(2)}, u32[]{:S(2)}) async-start(f32[1,1024,1024]{1,0,2:T(1,128)} %copy.13), calls=%async_computation | async-start | bytes 8388608 | tf_op jit(solution)/shard_map/all_to_all | solution.py:60
  69.8 0.8 dynamic-update-slice.3
  70.6 49.3 %all-reduce = s32[8]{0:T(128)S(1)} all-reduce(s32[8]{0:T(128)S(1)} %dynamic-update-slice.3), channel_id=1, replica_groups=mesh['wide'=8,'narrow'=4] {'wide'}, use_global_device_ids=true, to_apply=%add | all-reduce | flops 8 | bytes 64
  119.9 5.2 %copy.17 = f32[1,1024,1024]{1,2,0:T(8,128)} copy(f32[1,1024,1024]{1,0,2:T(1,128)} %all-to-all-done) | data formatting | bytes 8388608
  125.0 5.4 %copy.16 = f32[1,1024,8,128]{3,2,1,0:T(8,128)} copy(f32[1,1024,8,128]{1,3,2,0:T(8,128)} %bitcast.70) | data formatting | bytes 8388608 | tf_op jit(solution)/shard_map/all_to_all | solution.py:60
  130.4 5.6 %fusion = f32[4,1024,128]{2,0,1:T(4,128)} fusion(f32[1,1024,8,128]{3,2,1,0:T(8,128)} %copy.16, s32[8]{0:T(128)S(1)} %all-reduce), kind=kOutput, calls=%fused_computation | convolution fusion | flops 50331680 | bytes 6291488 | tf_op jit(solution)/shard_map/bw,bij->wij/dot_general | solution.py:26
  138.3 1.3 fusion.5
  139.7 79.8 %all-gather.1 = f32[32,4,1024]{2,1,0:T(4,128)S(1)} all-gather(f32[1,4,1024]{2,1,0:T(4,128)S(1)} %multiply_bitcast_fusion), channel_id=2, replica_groups=mesh['wide'=8,'narrow'=4] {'wide','narrow'}, dimensions={0}, use_global_device_ids=true | all-gather | bytes 540672 | tf_op jit(solution)/shard_map/all_gather | solution.py:57
  220.2 11.3 %all-reduce.4.cloned.1.call-done = f32[4,1024,128]{2,0,1:T(4,128)} async-done(((f32[4,1024,128]{2,0,1:T(4,128)}), f32[4,1024,128]{2,0,1:T(4,128)}) %all-reduce.4.cloned.1.call-update) | async-done | bytes 2097168
  231.5 1.1 constant_dynamic-slice_fusion
  232.6 0.8 copy.15
  (23 shorter events, 3.2 us)
Async XLA Ops:
  7.2 26.1 %copy-start = (f32[1,512]{1,0:T(1,128)S(1)}, f32[1,512]{1,0:T(1,128)}, u32[]{:S(2)}) copy-start(f32[1,512]{1,0:T(1,128)} %param.8) | copy-start | bytes 6148
  39.8 3.7 %copy-start.1 = (f32[1,512,1024]{2,1,0:T(8,128)S(1)}, f32[1,512,1024]{2,1,0:T(8,128)}, u32[]{:S(2)}) copy-start(f32[1,512,1024]{2,1,0:T(8,128)} %param.7) | copy-start | bytes 6291460
  63.2 6.0 %copy-start.3 = (u32[32]{0:T(128)S(1)}, u32[32]{0:T(128)}, u32[]{:S(2)}) copy-start(u32[32]{0:T(128)} %constant.68) | copy-start | bytes 388
  63.2 56.7 %all-to-all-start = ((f32[1,1024,1024]{1,0,2:T(1,128)}), f32[1,1024,1024]{1,0,2:T(1,128)}, u32[]{:S(2)}, u32[]{:S(2)}) async-start(f32[1,1024,1024]{1,0,2:T(1,128)} %copy.13), calls=%async_computation | async-start | bytes 8388608 | tf_op jit(solution)/shard_map/all_to_all | solution.py:60
  68.5 163.0 %all-reduce.4.cloned.1.call-start = ((), (), s32[]{:S(2)}) async-start(), calls=%async_computation.1 | async-start | bytes 4194304
  136.0 0.7 copy-start.2
Sparse Core Ops, SparseCore 0:
  136.1 95.3 all-reduce.3
